TPU v7x, 256 devices: a whole 4x4x8 slice. The times are simulated.
256 devices in a mesh: ctx: 32 (over z, y), head: 8 (over x, core).
Axes of the slice: x: 4, y: 4, z: 8, core: 2. Of those that a mesh axis runs over, the one named last changes fastest.
Arguments:
- query_input: bfloat16 [16384, 4096], P(('ctx', 'head')), may hold values from -6 to 6
- key_input: bfloat16 [16384, 4096], P(('ctx', 'head')), may hold values from -6 to 6
- value_input: bfloat16 [16384, 4096], P(('ctx', 'head')), may hold values from -6 to 6
- cotangent: bfloat16 [16384, 4096], P(('ctx', 'head')), may hold values from -6 to 6
- level_codes: int32 [32, 15, 16384], P('head', None, 'ctx'), may hold values from 0 to 15
Outputs:
- attended: bfloat16 [16384, 4096], P(('ctx', 'head'))
- grad_queries: bfloat16 [16384, 4096], P(('ctx', 'head'))
- grad_keys: bfloat16 [16384, 4096], P(('ctx', 'head'))
- grad_values: bfloat16 [16384, 4096], P(('ctx', 'head'))
All inputs are finite; a program needn't handle non-finite values.
Results may differ from a plain program's by a relative error of at most 0.0074.
Values may be sent and summed in bfloat16 or wider, within the bound.
A program may use at most 128 MiB of HBM per device.

v0:
```python
import jax
import jax.numpy as jnp
from jax import lax
from jax.sharding import PartitionSpec as P


def swapped(block, axis, stride):
    count = lax.axis_size(axis)
    route = []
    for low in range(count):
        high = low | 1 << stride
        if high != low and high < count:
            route += [(low, high), (high, low)]
    return lax.ppermute(block, axis, route)


def for_sending(x):

    def short(part):
        return part.astype(jnp.bfloat16) if part.dtype == jnp.float32 else part

    return jax.tree.map(short, x)


def level_gain(level):
    if level == 0:
        return 1.0
    return 2.0 ** (-(level - 1) / 2.0)


def on_device(query_input, key_input, value_input, cotangent, level_codes):
    query_rows, key_rows, value_rows, cot_rows = (
        lax.all_to_all(query_input, "head", split_axis=1, concat_axis=0, tiled=True),
        lax.all_to_all(key_input, "head", split_axis=1, concat_axis=0, tiled=True),
        lax.all_to_all(value_input, "head", split_axis=1, concat_axis=0, tiled=True),
        lax.all_to_all(cotangent, "head", split_axis=1, concat_axis=0, tiled=True),
    )
    head_count = level_codes.shape[0]
    total_levels = level_codes.shape[1]
    length = query_rows.shape[0]
    head_dim = query_rows.shape[1] // head_count
    tok_bits = length.bit_length() - 1
    ctx_bits = total_levels - tok_bits - 1
    score_scale = head_dim ** (-0.5)
    head_shape = (length, head_count, head_dim)
    query_heads = query_rows.reshape(head_shape)
    key_heads = key_rows.reshape(head_shape)
    value_heads = value_rows.reshape(head_shape)
    cot_heads = cot_rows.reshape(head_shape)
    code_weights = level_codes.astype(jnp.float32) / 8.0
    my_block = lax.axis_index("ctx")
    cross_scale = jnp.stack(
        [
            code_weights[:, tok_bits + 1 + bit_index, :]
            * (score_scale * level_gain(tok_bits + 1 + bit_index))
            * (my_block // 2**bit_index % 2).astype(jnp.float32)
            for bit_index in range(ctx_bits)
        ]
    )
    row_scale = jnp.transpose(cross_scale, (0, 2, 1))
    block_state = jnp.einsum(
        "phd,phe->hde", key_heads, value_heads, preferred_element_type=jnp.float32
    )
    scaled_cot = (row_scale[..., None] * cot_heads[None]).astype(jnp.bfloat16)
    grad_state = jnp.einsum(
        "phd,bphe->bhde", query_heads, scaled_cot, preferred_element_type=jnp.float32
    )
    running = block_state
    bucket_list = []
    for bit_index in range(ctx_bits):
        partner = swapped(running.astype(jnp.bfloat16), "ctx", bit_index).astype(running.dtype)
        bit_set = (my_block // 2**bit_index % 2).astype(jnp.float32)
        bucket_list.append(bit_set * partner)
        running = running + partner
    bucket_sums = jnp.stack(bucket_list)
    bucket = bucket_sums.astype(jnp.bfloat16)
    carried = [grad_state[level_index] for level_index in range(ctx_bits)]
    pulled = jnp.zeros((head_count, head_dim, head_dim), jnp.float32)
    for bit_index in range(ctx_bits):
        partner = swapped(for_sending(jnp.stack(carried)), "ctx", bit_index)
        bit_clear = 1.0 - (my_block // 2**bit_index % 2).astype(jnp.float32)
        pulled = pulled + bit_clear * partner[0]
        carried = [
            carried[level_index + 1] + partner[level_index + 1]
            for level_index in range(len(carried) - 1)
        ]
    pulled_half = pulled.astype(jnp.bfloat16)
    block_rows = min(512, length)
    steps_count = length // block_rows
    places = jnp.arange(length, dtype=jnp.int32)

    def row_step(carried_grads, block_index):
        key_grad, value_grad = carried_grads
        first_row = block_index * block_rows
        rows_at = first_row + jnp.arange(block_rows, dtype=jnp.int32)
        levels = jnp.zeros((block_rows, length), jnp.int32)
        for bit_index in range(tok_bits):
            levels = levels + (
                rows_at[:, None] // 2**bit_index != places[None, :] // 2**bit_index
            ).astype(jnp.int32)
        weight = jnp.zeros((head_count, block_rows, length), jnp.float32)
        for level_index in range(tok_bits + 1):
            weight = jnp.where(
                (levels == level_index)[None],
                code_weights[:, level_index, :, None] * level_gain(level_index),
                weight,
            )
        weight = jnp.where((places[None, :] <= rows_at[:, None])[None], weight, 0.0)
        scores = jnp.einsum(
            "phd,shd->hps", query_heads, key_heads, preferred_element_type=jnp.float32
        )
        attention = (score_scale * weight * scores).astype(jnp.bfloat16)
        local_out = jnp.einsum(
            "hps,she->phe", attention, value_heads, preferred_element_type=jnp.float32
        )
        dots = jnp.einsum(
            "phe,she->hps", cot_heads, value_heads, preferred_element_type=jnp.float32
        )
        score_grads = (score_scale * weight * dots).astype(jnp.bfloat16)
        local_qgrad = jnp.einsum(
            "hps,shd->phd", score_grads, key_heads, preferred_element_type=jnp.float32
        )
        key_grad = key_grad + jnp.einsum(
            "hps,phd->shd", score_grads, query_heads, preferred_element_type=jnp.float32
        )
        value_grad = value_grad + jnp.einsum(
            "hps,phe->she", attention, cot_heads, preferred_element_type=jnp.float32
        )
        return ((key_grad, value_grad), (local_out, local_qgrad))

    zero_grads = jnp.zeros(head_shape, jnp.float32)
    (key_local, value_local), (local_out, local_qgrad) = lax.scan(
        row_step, (zero_grads, zero_grads), jnp.arange(steps_count, dtype=jnp.int32)
    )
    local_out = local_out.reshape(head_shape)
    local_qgrad = local_qgrad.reshape(head_shape)
    cross_out = jnp.sum(
        row_scale[..., None]
        * jnp.einsum("phd,bhde->bphe", query_heads, bucket, preferred_element_type=jnp.float32),
        axis=0,
    )
    cross_qgrad = jnp.sum(
        row_scale[..., None]
        * jnp.einsum("phe,bhde->bphd", cot_heads, bucket, preferred_element_type=jnp.float32),
        axis=0,
    )
    flat_shape = (length, head_count * head_dim)
    attended = (local_out + cross_out).astype(jnp.bfloat16).reshape(flat_shape)
    grad_query = (local_qgrad + cross_qgrad).astype(jnp.bfloat16).reshape(flat_shape)
    grad_key = (
        (
            key_local
            + jnp.einsum(
                "phe,hde->phd", value_heads, pulled_half, preferred_element_type=jnp.float32
            )
        )
        .astype(jnp.bfloat16)
        .reshape(flat_shape)
    )
    grad_value = (
        (
            value_local
            + jnp.einsum("phd,hde->phe", key_heads, pulled_half, preferred_element_type=jnp.float32)
        )
        .astype(jnp.bfloat16)
        .reshape(flat_shape)
    )
    return (
        lax.all_to_all(attended, "head", split_axis=0, concat_axis=1, tiled=True),
        lax.all_to_all(grad_query, "head", split_axis=0, concat_axis=1, tiled=True),
        lax.all_to_all(grad_key, "head", split_axis=0, concat_axis=1, tiled=True),
        lax.all_to_all(grad_value, "head", split_axis=0, concat_axis=1, tiled=True),
    )


def solution(mesh):
    return jax.shard_map(
        on_device,
        mesh=mesh,
        in_specs=(
            P(("ctx", "head"), None),
            P(("ctx", "head"), None),
            P(("ctx", "head"), None),
            P(("ctx", "head"), None),
            P("head", None, "ctx"),
        ),
        out_specs=(
            P(("ctx", "head"), None),
            P(("ctx", "head"), None),
            P(("ctx", "head"), None),
            P(("ctx", "head"), None),
        ),
        check_vma=False,
    )
```

profile of v0, /device:TPU:1, one launch (start us, length us, event | category | flops | bytes accessed | tf_op | source)
XLA Modules:
  0.0 212.4 jit_solution(3397119964379641207)
XLA Ops:
  0.7 1.9 copy.194
  2.6 6.7 %all-to-all-start.2 = ((bf16[64,8,512]{2,0,1:T(8,128)(2,1)}), bf16[64,8,512]{2,0,1:T(8,128)(2,1)S(1)}, u32[]{:S(2)}, u32[]{:S(2)}) async-start(bf16[64,8,512]{2,0,1:T(8,128)(2,1)} %bitcast.140), calls=%async_computation.2 | async-start | bytes 1048576 | tf_op jit(solution)/shard_map/all_to_all | solution.py:35
  9.5 0.8 copy.195
  10.4 8.3 %all-to-all-done.2 = bf16[64,8,512]{2,0,1:T(8,128)(2,1)S(1)} async-done(((bf16[64,8,512]{2,0,1:T(8,128)(2,1)}), bf16[64,8,512]{2,0,1:T(8,128)(2,1)S(1)}, u32[]{:S(2)}, u32[]{:S(2)}) %all-to-all-start.2) | async-done | bytes 524320 | tf_op jit(solution)/shard_map/all_to_all | solution.py:35
  18.7 4.4 %all-to-all-start.1 = ((bf16[64,8,512]{2,0,1:T(8,128)(2,1)}), bf16[64,8,512]{2,0,1:T(8,128)(2,1)S(1)}, u32[]{:S(2)}, u32[]{:S(2)}) async-start(bf16[64,8,512]{2,0,1:T(8,128)(2,1)} %bitcast.141), calls=%async_computation.1 | async-start | bytes 1048576 | tf_op jit(solution)/shard_map/all_to_all | solution.py:34
  23.7 0.8 copy.196
  24.6 0.8 copy.193
  25.5 6.9 %all-to-all-done.1 = bf16[64,8,512]{2,0,1:T(8,128)(2,1)S(1)} async-done(((bf16[64,8,512]{2,0,1:T(8,128)(2,1)}), bf16[64,8,512]{2,0,1:T(8,128)(2,1)S(1)}, u32[]{:S(2)}, u32[]{:S(2)}) %all-to-all-start.1) | async-done | bytes 524320 | tf_op jit(solution)/shard_map/all_to_all | solution.py:34
  32.5 4.4 %all-to-all-start = ((bf16[64,8,512]{2,0,1:T(8,128)(2,1)}), bf16[64,8,512]{2,0,1:T(8,128)(2,1)S(1)}, u32[]{:S(2)}, u32[]{:S(2)}) async-start(bf16[64,8,512]{2,0,1:T(8,128)(2,1)} %bitcast.142), calls=%async_computation | async-start | bytes 1048576 | tf_op jit(solution)/shard_map/all_to_all | solution.py:33
  36.8 3.9 %broadcast_compare_fusion.9 = (pred[512,512]{1,0:T(8,128)(4,1)}, pred[512,512]{1,0:T(8,128)(4,1)}, pred[512,512]{1,0:T(8,128)(4,1)}, pred[512,512]{1,0:T(8,128)(...) fusion(s32[512]{0:T(512)S(1)} %get-tuple-element.70, ...), kind=kLoop, calls=%fused_computation.46 | loop fusion | flops 9437184 | bytes 2637824 | tf_op jit(solution)/shard_map/while/body/eval_jaxpr/eq | solution.py:104
  40.8 5.4 %all-to-all-done = bf16[64,8,512]{2,0,1:T(8,128)(2,1)S(1)} async-done(((bf16[64,8,512]{2,0,1:T(8,128)(2,1)}), bf16[64,8,512]{2,0,1:T(8,128)(2,1)S(1)}, u32[]{:S(2)}, u32[]{:S(2)}) %all-to-all-start) | async-done | bytes 524320 | tf_op jit(solution)/shard_map/all_to_all | solution.py:33
  46.2 4.4 %all-to-all-start.4 = ((bf16[64,8,512]{2,0,1:T(8,128)(2,1)}), bf16[64,8,512]{2,0,1:T(8,128)(2,1)S(1)}, u32[]{:S(2)}, u32[]{:S(2)}) async-start(bf16[64,8,512]{2,0,1:T(8,128)(2,1)} %bitcast.139), calls=%async_computation.4 | async-start | bytes 1048576 | tf_op jit(solution)/shard_map/all_to_all | solution.py:36
  50.9 1.0 fusion.89
  52.4 0.9 reshape.3029
  53.3 6.6 %all-to-all-done.4 = bf16[64,8,512]{2,0,1:T(8,128)(2,1)S(1)} async-done(((bf16[64,8,512]{2,0,1:T(8,128)(2,1)}), bf16[64,8,512]{2,0,1:T(8,128)(2,1)S(1)}, u32[]{:S(2)}, u32[]{:S(2)}) %all-to-all-start.4) | async-done | bytes 524320 | tf_op jit(solution)/shard_map/all_to_all | solution.py:36
  60.1 1.3 copy.112
  61.6 7.4 %multiply_convert_fusion.1 = bf16[4,512,512]{2,1,0:T(8,128)(2,1)} fusion(f32[4,512]{1,0:T(4,128)S(1)} %get-tuple-element.47, f32[4,512]{1,0:T(4,128)S(1)} %get-tuple-element.48, f32[4,512]{1,0:T(4,128)S(1)} %get-tuple-element.49, f32[4,512]{1,0:T(4,128)S(1)} %get-tuple-element.50, f32[4,512]{1,0:T(4,128)S(1)} %get-tuple-element.51, ...), kind=kOutput, calls=%fused_computation.5 | convolution fusion | flops 283115520 | bytes 6111232 | tf_op jit(solution)/shard_map/while/body/eval_jaxpr/phe,she->hps/dot_general | solution.py:116
  69.1 6.4 %multiply_convert_fusion.2 = bf16[4,512,512]{2,1,0:T(8,128)(2,1)S(1)} fusion(f32[4,512]{1,0:T(4,128)S(1)} %get-tuple-element.47, f32[4,512]{1,0:T(4,128)} %copy-done.25, f32[4,512]{1,0:T(4,128)} %copy-done.26, f32[4,512]{1,0:T(4,128)} %copy-done.27, f32[4,512]{1,0:T(4,128)} %copy-done.28, f32[4,512]{1,0:T(4,128)} %copy-done.29, f32[4,512]{1,0:T(4,128)} %copy-done.30, ...), kind=kOutput, calls=%fused_computation.6 | convolution fusion | flops 283115520 | bytes 6111232 | tf_op jit(solution)/shard_map/while/body/eval_jaxpr/phd,shd->hps/dot_general | solution.py:109
  75.5 0.9 fusion.90
  77.0 2.7 %collective-permute-start.1 = (bf16[4,128,128]{2,1,0:T(8,128)(2,1)S(1)}, bf16[4,128,128]{2,1,0:T(8,128)(2,1)S(1)}, u32[]{:S(2)}, u32[]{:S(2)}) collective-permute-start(bf16[4,128,128]{2,1,0:T(8,128)(2,1)S(1)} %fusion.40), channel_id=1, source_target_pairs={{0,16},{16,0},{8,24},{24,8},{32,48},{48,32},{40,56},{56,40},{64,80... | collective-permute-start | bytes 393224 | tf_op jit(solution)/shard_map/ppermute | solution.py:14
  79.7 16.2 %collective-permute-done.1 = bf16[4,128,128]{2,1,0:T(8,128)(2,1)S(1)} collective-permute-done((bf16[4,128,128]{2,1,0:T(8,128)(2,1)S(1)}, bf16[4,128,128]{2,1,0:T(8,128)(2,1)S(1)}, u32[]{:S(2)}, u32[]{:S(2)}) %collective-permute-start.1) | collective-permute-done | bytes 131104 | tf_op jit(solution)/shard_map/ppermute | solution.py:14
  96.0 1.7 collective-permute-start.2
  97.8 2.3 %collective-permute-done.2 = bf16[4,128,128]{2,1,0:T(8,128)(2,1)S(1)} collective-permute-done((bf16[4,128,128]{2,1,0:T(8,128)(2,1)S(1)}, bf16[4,128,128]{2,1,0:T(8,128)(2,1)S(1)}, u32[]{:S(2)}, u32[]{:S(2)}) %collective-permute-start.2) | collective-permute-done | bytes 131104 | tf_op jit(solution)/shard_map/ppermute | solution.py:14
  100.2 3.1 %collective-permute-start.3 = (bf16[4,128,128]{2,1,0:T(8,128)(2,1)S(1)}, bf16[4,128,128]{2,1,0:T(8,128)(2,1)S(1)}, u32[]{:S(2)}, u32[]{:S(2)}) collective-permute-start(bf16[4,128,128]{2,1,0:T(8,128)(2,1)S(1)} %fusion.41), channel_id=1, source_target_pairs={{0,64},{64,0},{8,72},{72,8},{16,80},{80,16},{24,88},{88,24},{32,96... | collective-permute-start | bytes 393224 | tf_op jit(solution)/shard_map/ppermute | solution.py:14
  103.3 3.7 %collective-permute-done.3 = bf16[4,128,128]{2,1,0:T(8,128)(2,1)S(1)} collective-permute-done((bf16[4,128,128]{2,1,0:T(8,128)(2,1)S(1)}, bf16[4,128,128]{2,1,0:T(8,128)(2,1)S(1)}, u32[]{:S(2)}, u32[]{:S(2)}) %collective-permute-start.3) | collective-permute-done | bytes 131104 | tf_op jit(solution)/shard_map/ppermute | solution.py:14
  107.1 6.2 %collective-permute-start.4 = (bf16[4,128,128]{2,1,0:T(8,128)(2,1)S(1)}, bf16[4,128,128]{2,1,0:T(8,128)(2,1)S(1)}, u32[]{:S(2)}, u32[]{:S(2)}) collective-permute-start(bf16[4,128,128]{2,1,0:T(8,128)(2,1)S(1)} %fusion.36), channel_id=1, source_target_pairs={{0,128},{128,0},{8,136},{136,8},{16,144},{144,16},{24,152},{152,24... | collective-permute-start | bytes 393224 | tf_op jit(solution)/shard_map/ppermute | solution.py:14
  114.2 0.9 pad_maximum_fusion
  115.8 0.8 copy-done.24
  116.7 1.9 fusion.1
  118.6 2.5 %copy.98 = f32[512,4,128]{2,0,1:T(8,128)} copy(f32[512,4,128]{0,2,1:T(8,128)} %fusion.1) | data formatting | bytes 2097152 | tf_op jit(solution)/shard_map/reduce_sum | solution.py:137
  121.2 4.5 %collective-permute-done.6 = bf16[4,4,128,128]{2,3,0,1:T(8,128)(2,1)} collective-permute-done((bf16[4,4,128,128]{2,3,0,1:T(8,128)(2,1)}, bf16[4,4,128,128]{2,3,0,1:T(8,128)(2,1)}, u32[]{:S(2)}, u32[]{:S(2)}) %collective-permute-start.6) | collective-permute-done | bytes 524320 | tf_op jit(solution)/shard_map/ppermute | solution.py:14
  125.6 1.5 add_convert_fusion.3
  127.1 0.9 pad_maximum_fusion.1
  128.7 1.2 copy.99
  129.9 2.0 convert_element_type.688
  131.9 9.6 %all-to-all-start.3 = ((bf16[8,64,512]{2,1,0:T(8,128)(2,1)}), bf16[8,64,512]{2,1,0:T(8,128)(2,1)}, u32[]{:S(2)}, u32[]{:S(2)}) async-start(bf16[8,64,512]{2,1,0:T(8,128)(2,1)} %convert_element_type.688), calls=%async_computation.3 | async-start | bytes 1048576 | tf_op jit(solution)/shard_map/all_to_all | solution.py:169
  141.6 3.2 %fusion = f32[512,4,128]{0,2,1:T(8,128)} fusion(f32[5,512,4]{1,0,2:T(8,128)} %copy.93, bf16[5,4,128,128]{3,2,1,0:T(8,128)(2,1)} %copy-done.24, bf16[512,4,128,1]{2,1,0,3:T(4,128)(2,1)} %bitcast.143), kind=kOutput, calls=%fused_computation.1 | convolution fusion | flops 337903616 | bytes 2269184 | tf_op jit(solution)/shard_map/phe,bhde->bphd/dot_general | solution.py:144
  144.8 2.5 %copy.107 = f32[512,4,128]{2,0,1:T(8,128)} copy(f32[512,4,128]{0,2,1:T(8,128)} %fusion) | data formatting | bytes 2097152 | tf_op jit(solution)/shard_map/reduce_sum | solution.py:142
  147.3 1.6 add_convert_fusion.2
  149.6 3.1 %collective-permute-start.8 = (bf16[2,4,128,128]{2,3,0,1:T(8,128)(2,1)}, bf16[2,4,128,128]{2,3,0,1:T(8,128)(2,1)}, u32[]{:S(2)}, u32[]{:S(2)}) collective-permute-start(bf16[2,4,128,128]{2,3,0,1:T(8,128)(2,1)} %pad_maximum_fusion.2), channel_id=1, source_target_pairs={{0,64},{64,0},{8,72},{72,8},{16,80},{80,16},{24,88},{88,24},{32,96... | collective-permute-start | bytes 786440 | tf_op jit(solution)/shard_map/ppermute | solution.py:14
  152.7 2.0 fusion.10
  154.7 1.2 copy.108
  155.9 2.0 convert_element_type.691
  157.9 7.3 %collective-permute-done.8 = bf16[2,4,128,128]{2,3,0,1:T(8,128)(2,1)} collective-permute-done((bf16[2,4,128,128]{2,3,0,1:T(8,128)(2,1)}, bf16[2,4,128,128]{2,3,0,1:T(8,128)(2,1)}, u32[]{:S(2)}, u32[]{:S(2)}) %collective-permute-start.8) | collective-permute-done | bytes 262176 | tf_op jit(solution)/shard_map/ppermute | solution.py:14
  165.2 1.9 add_convert_fusion.1
  167.1 1.4 collective-permute-start.9
  168.5 5.4 %all-to-all-start.5 = ((bf16[8,64,512]{2,1,0:T(8,128)(2,1)}), bf16[8,64,512]{2,1,0:T(8,128)(2,1)}, u32[]{:S(2)}, u32[]{:S(2)}) async-start(bf16[8,64,512]{2,1,0:T(8,128)(2,1)} %convert_element_type.691), calls=%async_computation.5 | async-start | bytes 1048576 | tf_op jit(solution)/shard_map/all_to_all | solution.py:170
  173.9 2.6 %convolution_bitcast_fusion.1 = f32[512,4,128]{2,0,1:T(8,128)S(1)} fusion(bf16[4,512,512]{2,1,0:T(8,128)(2,1)} %multiply_convert_fusion.1, bf16[512,4,128]{2,1,0:T(4,128)(2,1)} %reshape.3029), kind=kOutput, calls=%fused_computation.13 | convolution fusion | flops 268435456 | bytes 3670016 | tf_op jit(solution)/shard_map/while/body/eval_jaxpr/hps,phd->shd/dot_general | solution.py:123
  176.4 1.4 collective-permute-done.9
  177.8 1.5 fusion.13
  179.3 1.2 copy.117
  180.5 2.0 all_to_all.118
  182.5 0.8 all-to-all-done.5
  183.3 5.0 %all-to-all-start.6 = ((bf16[8,64,512]{2,1,0:T(8,128)(2,1)}), bf16[8,64,512]{2,1,0:T(8,128)(2,1)}, u32[]{:S(2)}, u32[]{:S(2)}) async-start(bf16[8,64,512]{2,1,0:T(8,128)(2,1)} %all_to_all.118), calls=%async_computation.6 | async-start | bytes 1048576 | tf_op jit(solution)/shard_map/all_to_all | solution.py:171
  188.3 0.9 convolution_bitcast_fusion
  189.2 1.5 fusion.12
  191.1 1.0 all_to_all.122
  192.1 5.7 %all-to-all-done.6 = bf16[8,64,512]{2,1,0:T(8,128)(2,1)} async-done(((bf16[8,64,512]{2,1,0:T(8,128)(2,1)}), bf16[8,64,512]{2,1,0:T(8,128)(2,1)}, u32[]{:S(2)}, u32[]{:S(2)}) %all-to-all-start.6) | async-done | bytes 524320 | tf_op jit(solution)/shard_map/all_to_all | solution.py:171
  197.8 4.4 %all-to-all-start.7 = ((bf16[8,64,512]{2,1,0:T(8,128)(2,1)}), bf16[8,64,512]{2,1,0:T(8,128)(2,1)S(1)}, u32[]{:S(2)}, u32[]{:S(2)}) async-start(bf16[8,64,512]{2,1,0:T(8,128)(2,1)} %all_to_all.122), calls=%async_computation.7 | async-start | bytes 1048576 | tf_op jit(solution)/shard_map/all_to_all | solution.py:172
  202.2 1.9 copy.145
  204.1 1.9 copy.146
  205.9 1.9 copy.147
  207.8 3.7 %all-to-all-done.7 = bf16[8,64,512]{2,1,0:T(8,128)(2,1)S(1)} async-done(((bf16[8,64,512]{2,1,0:T(8,128)(2,1)}), bf16[8,64,512]{2,1,0:T(8,128)(2,1)S(1)}, u32[]{:S(2)}, u32[]{:S(2)}) %all-to-all-start.7) | async-done | bytes 524320 | tf_op jit(solution)/shard_map/all_to_all | solution.py:172
  211.6 0.8 copy.148
  (103 shorter events, 6.3 us)
Async XLA Ops:
  0.6 8.7 %copy-start.22 = (s32[4,15,512]{2,0,1:T(4,128)S(1)}, s32[4,15,512]{2,0,1:T(4,128)}, u32[]{:S(2)}) copy-start(s32[4,15,512]{2,0,1:T(4,128)} %param.9) | copy-start | bytes 368644
  0.6 8.9 %copy-start.8 = (bf16[64,4096]{1,0:T(8,128)(2,1)S(1)}, bf16[64,4096]{1,0:T(8,128)(2,1)}, u32[]{:S(2)}) copy-start(bf16[64,4096]{1,0:T(8,128)(2,1)} %param.6) | copy-start | bytes 1572868
  2.6 21.1 %copy-start.9 = (bf16[64,4096]{1,0:T(8,128)(2,1)S(1)}, bf16[64,4096]{1,0:T(8,128)(2,1)}, u32[]{:S(2)}) copy-start(bf16[64,4096]{1,0:T(8,128)(2,1)} %param.5) | copy-start | bytes 1572868
  2.6 16.1 %all-to-all-start.2 = ((bf16[64,8,512]{2,0,1:T(8,128)(2,1)}), bf16[64,8,512]{2,0,1:T(8,128)(2,1)S(1)}, u32[]{:S(2)}, u32[]{:S(2)}) async-start(bf16[64,8,512]{2,0,1:T(8,128)(2,1)} %bitcast.140), calls=%async_computation.2 | async-start | bytes 1048576 | tf_op jit(solution)/shard_map/all_to_all | solution.py:35
  9.3 15.2 %copy-start.10 = (bf16[64,4096]{1,0:T(8,128)(2,1)S(1)}, bf16[64,4096]{1,0:T(8,128)(2,1)}, u32[]{:S(2)}) copy-start(bf16[64,4096]{1,0:T(8,128)(2,1)} %param.8) | copy-start | bytes 1572868
  18.7 13.7 %all-to-all-start.1 = ((bf16[64,8,512]{2,0,1:T(8,128)(2,1)}), bf16[64,8,512]{2,0,1:T(8,128)(2,1)S(1)}, u32[]{:S(2)}, u32[]{:S(2)}) async-start(bf16[64,8,512]{2,0,1:T(8,128)(2,1)} %bitcast.141), calls=%async_computation.1 | async-start | bytes 1048576 | tf_op jit(solution)/shard_map/all_to_all | solution.py:34
  25.5 35.9 %copy-start.11 = (pred[512,512]{1,0:T(8,128)(4,1)}, pred[512,512]{1,0:T(8,128)(4,1)S(1)}, u32[]{:S(2)}) copy-start(pred[512,512]{1,0:T(8,128)(4,1)S(1)} %iota_compare_fusion.1) | copy-start | bytes 786436
  32.5 13.7 %all-to-all-start = ((bf16[64,8,512]{2,0,1:T(8,128)(2,1)}), bf16[64,8,512]{2,0,1:T(8,128)(2,1)S(1)}, u32[]{:S(2)}, u32[]{:S(2)}) async-start(bf16[64,8,512]{2,0,1:T(8,128)(2,1)} %bitcast.142), calls=%async_computation | async-start | bytes 1048576 | tf_op jit(solution)/shard_map/all_to_all | solution.py:33
  46.2 13.7 %all-to-all-start.4 = ((bf16[64,8,512]{2,0,1:T(8,128)(2,1)}), bf16[64,8,512]{2,0,1:T(8,128)(2,1)S(1)}, u32[]{:S(2)}, u32[]{:S(2)}) async-start(bf16[64,8,512]{2,0,1:T(8,128)(2,1)} %bitcast.139), calls=%async_computation.4 | async-start | bytes 1048576 | tf_op jit(solution)/shard_map/all_to_all | solution.py:36
  50.6 10.8 %copy-start.25 = (f32[4,512]{1,0:T(4,128)}, f32[4,512]{1,0:T(4,128)S(1)}, u32[]{:S(2)}) copy-start(f32[4,512]{1,0:T(4,128)S(1)} %get-tuple-element.48) | copy-start | bytes 24580
  50.6 10.8 %copy-start.26 = (f32[4,512]{1,0:T(4,128)}, f32[4,512]{1,0:T(4,128)S(1)}, u32[]{:S(2)}) copy-start(f32[4,512]{1,0:T(4,128)S(1)} %get-tuple-element.49) | copy-start | bytes 24580
  50.6 10.8 %copy-start.27 = (f32[4,512]{1,0:T(4,128)}, f32[4,512]{1,0:T(4,128)S(1)}, u32[]{:S(2)}) copy-start(f32[4,512]{1,0:T(4,128)S(1)} %get-tuple-element.50) | copy-start | bytes 24580
  50.6 10.8 %copy-start.28 = (f32[4,512]{1,0:T(4,128)}, f32[4,512]{1,0:T(4,128)S(1)}, u32[]{:S(2)}) copy-start(f32[4,512]{1,0:T(4,128)S(1)} %get-tuple-element.51) | copy-start | bytes 24580
  50.6 10.8 %copy-start.29 = (f32[4,512]{1,0:T(4,128)}, f32[4,512]{1,0:T(4,128)S(1)}, u32[]{:S(2)}) copy-start(f32[4,512]{1,0:T(4,128)S(1)} %get-tuple-element.52) | copy-start | bytes 24580
  50.6 10.8 %copy-start.30 = (f32[4,512]{1,0:T(4,128)}, f32[4,512]{1,0:T(4,128)S(1)}, u32[]{:S(2)}) copy-start(f32[4,512]{1,0:T(4,128)S(1)} %get-tuple-element.53) | copy-start | bytes 24580
  50.6 10.8 %copy-start.31 = (f32[4,512]{1,0:T(4,128)}, f32[4,512]{1,0:T(4,128)S(1)}, u32[]{:S(2)}) copy-start(f32[4,512]{1,0:T(4,128)S(1)} %get-tuple-element.54) | copy-start | bytes 24580
  50.6 10.8 %copy-start.32 = (f32[4,512]{1,0:T(4,128)}, f32[4,512]{1,0:T(4,128)S(1)}, u32[]{:S(2)}) copy-start(f32[4,512]{1,0:T(4,128)S(1)} %get-tuple-element.55) | copy-start | bytes 24580
  51.9 25.0 %collective-permute-start = (bf16[4,128,128]{2,1,0:T(8,128)(2,1)}, bf16[4,128,128]{2,1,0:T(8,128)(2,1)S(1)}, u32[]{:S(2)}, u32[]{:S(2)}) collective-permute-start(bf16[4,128,128]{2,1,0:T(8,128)(2,1)} %get-tuple-element.66), channel_id=1, source_target_pairs={{0,8},{8,0},{16,24},{24,16},{32,40},{40,32},{48,56},{56,48},{64,72... | collective-permute-start | bytes 393224 | tf_op jit(solution)/shard_map/ppermute | solution.py:14
  60.1 1.4 copy-start.2
  61.5 7.5 %copy-start.6 = (bf16[512,4,128]{2,1,0:T(4,128)(2,1)S(1)}, bf16[512,4,128]{2,1,0:T(4,128)(2,1)}, u32[]{:S(2)}) copy-start(bf16[512,4,128]{2,1,0:T(4,128)(2,1)} %reshape.3029) | copy-start | bytes 1572868
  61.5 7.5 %copy-start.12 = (pred[512,512]{1,0:T(8,128)(4,1)S(1)}, pred[512,512]{1,0:T(8,128)(4,1)}, u32[]{:S(2)}) copy-start(pred[512,512]{1,0:T(8,128)(4,1)} %get-tuple-element.56) | copy-start | bytes 786436
  61.5 7.5 %copy-start.13 = (pred[512,512]{1,0:T(8,128)(4,1)S(1)}, pred[512,512]{1,0:T(8,128)(4,1)}, u32[]{:S(2)}) copy-start(pred[512,512]{1,0:T(8,128)(4,1)} %get-tuple-element.57) | copy-start | bytes 786436
  61.5 7.5 %copy-start.14 = (pred[512,512]{1,0:T(8,128)(4,1)S(1)}, pred[512,512]{1,0:T(8,128)(4,1)}, u32[]{:S(2)}) copy-start(pred[512,512]{1,0:T(8,128)(4,1)} %get-tuple-element.58) | copy-start | bytes 786436
  61.5 7.5 %copy-start.15 = (pred[512,512]{1,0:T(8,128)(4,1)S(1)}, pred[512,512]{1,0:T(8,128)(4,1)}, u32[]{:S(2)}) copy-start(pred[512,512]{1,0:T(8,128)(4,1)} %get-tuple-element.59) | copy-start | bytes 786436
  61.5 7.5 %copy-start.16 = (pred[512,512]{1,0:T(8,128)(4,1)S(1)}, pred[512,512]{1,0:T(8,128)(4,1)}, u32[]{:S(2)}) copy-start(pred[512,512]{1,0:T(8,128)(4,1)} %get-tuple-element.60) | copy-start | bytes 786436
  61.5 7.5 %copy-start.17 = (pred[512,512]{1,0:T(8,128)(4,1)S(1)}, pred[512,512]{1,0:T(8,128)(4,1)}, u32[]{:S(2)}) copy-start(pred[512,512]{1,0:T(8,128)(4,1)} %get-tuple-element.61) | copy-start | bytes 786436
  61.5 7.5 %copy-start.18 = (pred[512,512]{1,0:T(8,128)(4,1)S(1)}, pred[512,512]{1,0:T(8,128)(4,1)}, u32[]{:S(2)}) copy-start(pred[512,512]{1,0:T(8,128)(4,1)} %get-tuple-element.62) | copy-start | bytes 786436
  61.5 7.5 %copy-start.19 = (pred[512,512]{1,0:T(8,128)(4,1)S(1)}, pred[512,512]{1,0:T(8,128)(4,1)}, u32[]{:S(2)}) copy-start(pred[512,512]{1,0:T(8,128)(4,1)} %get-tuple-element.63) | copy-start | bytes 786436
  61.6 7.5 %copy-start.20 = (pred[512,512]{1,0:T(8,128)(4,1)S(1)}, pred[512,512]{1,0:T(8,128)(4,1)}, u32[]{:S(2)}) copy-start(pred[512,512]{1,0:T(8,128)(4,1)} %get-tuple-element.64) | copy-start | bytes 786436
  61.6 7.5 %copy-start.21 = (pred[512,512]{1,0:T(8,128)(4,1)S(1)}, pred[512,512]{1,0:T(8,128)(4,1)}, u32[]{:S(2)}) copy-start(pred[512,512]{1,0:T(8,128)(4,1)} %get-tuple-element.65) | copy-start | bytes 786436
  69.1 6.4 %copy-start.7 = (f32[512,4,128]{0,2,1:T(8,128)S(1)}, f32[512,4,128]{0,2,1:T(8,128)}, u32[]{:S(2)}) copy-start(f32[512,4,128]{0,2,1:T(8,128)} %copy.112) | copy-start | bytes 3145732
  69.1 6.4 %copy-start.23 = (f32[5,512,4]{1,0,2:T(8,128)S(1)}, f32[5,512,4]{1,0,2:T(8,128)}, u32[]{:S(2)}) copy-start(f32[5,512,4]{1,0,2:T(8,128)} %copy.93) | copy-start | bytes 122884
  76.4 37.1 %copy-start.1 = (f32[5,4,128,128]{2,3,0,1:T(8,128)}, f32[5,4,128,128]{2,3,0,1:T(8,128)S(1)}, u32[]{:S(2)}) copy-start(f32[5,4,128,128]{2,3,0,1:T(8,128)S(1)} %get-tuple-element.69) | copy-start | bytes 3932164
  76.4 36.9 %collective-permute-start.5 = (bf16[5,4,128,128]{2,3,0,1:T(8,128)(2,1)S(1)}, bf16[5,4,128,128]{2,3,0,1:T(8,128)(2,1)S(1)}, u32[]{:S(2)}, u32[]{:S(2)}) collective-permute-start(bf16[5,4,128,128]{2,3,0,1:T(8,128)(2,1)S(1)} %get-tuple-element.68), channel_id=1, source_target_pairs={{0,8},{8,0},{16,24},{24,16},{32,40},{40,32},{48,56},{56,48},{64,72... | collective-permute-start | bytes 1966088 | tf_op jit(solution)/shard_map/ppermute | solution.py:14
  77.0 19.0 %collective-permute-start.1 = (bf16[4,128,128]{2,1,0:T(8,128)(2,1)S(1)}, bf16[4,128,128]{2,1,0:T(8,128)(2,1)S(1)}, u32[]{:S(2)}, u32[]{:S(2)}) collective-permute-start(bf16[4,128,128]{2,1,0:T(8,128)(2,1)S(1)} %fusion.40), channel_id=1, source_target_pairs={{0,16},{16,0},{8,24},{24,8},{32,48},{48,32},{40,56},{56,40},{64,80... | collective-permute-start | bytes 393224 | tf_op jit(solution)/shard_map/ppermute | solution.py:14
  96.0 4.1 %collective-permute-start.2 = (bf16[4,128,128]{2,1,0:T(8,128)(2,1)S(1)}, bf16[4,128,128]{2,1,0:T(8,128)(2,1)S(1)}, u32[]{:S(2)}, u32[]{:S(2)}) collective-permute-start(bf16[4,128,128]{2,1,0:T(8,128)(2,1)S(1)} %fusion.87), channel_id=1, source_target_pairs={{0,32},{32,0},{8,40},{40,8},{16,48},{48,16},{24,56},{56,24},{64,96... | collective-permute-start | bytes 393224 | tf_op jit(solution)/shard_map/ppermute | solution.py:14
  100.2 6.8 %collective-permute-start.3 = (bf16[4,128,128]{2,1,0:T(8,128)(2,1)S(1)}, bf16[4,128,128]{2,1,0:T(8,128)(2,1)S(1)}, u32[]{:S(2)}, u32[]{:S(2)}) collective-permute-start(bf16[4,128,128]{2,1,0:T(8,128)(2,1)S(1)} %fusion.41), channel_id=1, source_target_pairs={{0,64},{64,0},{8,72},{72,8},{16,80},{80,16},{24,88},{88,24},{32,96... | collective-permute-start | bytes 393224 | tf_op jit(solution)/shard_map/ppermute | solution.py:14
  107.1 8.7 %collective-permute-start.4 = (bf16[4,128,128]{2,1,0:T(8,128)(2,1)S(1)}, bf16[4,128,128]{2,1,0:T(8,128)(2,1)S(1)}, u32[]{:S(2)}, u32[]{:S(2)}) collective-permute-start(bf16[4,128,128]{2,1,0:T(8,128)(2,1)S(1)} %fusion.36), channel_id=1, source_target_pairs={{0,128},{128,0},{8,136},{136,8},{16,144},{144,16},{24,152},{152,24... | collective-permute-start | bytes 393224 | tf_op jit(solution)/shard_map/ppermute | solution.py:14
  113.3 0.9 copy-start.5
  115.0 10.6 %collective-permute-start.6 = (bf16[4,4,128,128]{2,3,0,1:T(8,128)(2,1)}, bf16[4,4,128,128]{2,3,0,1:T(8,128)(2,1)}, u32[]{:S(2)}, u32[]{:S(2)}) collective-permute-start(bf16[4,4,128,128]{2,3,0,1:T(8,128)(2,1)} %pad_maximum_fusion), channel_id=1, source_target_pairs={{0,16},{16,0},{8,24},{24,8},{32,48},{48,32},{40,56},{56,40},{64,80... | collective-permute-start | bytes 1572872 | tf_op jit(solution)/shard_map/ppermute | solution.py:14
  115.8 0.8 copy-start.24
  121.1 6.8 %copy-start.4 = (f32[512,4,128]{2,0,1:T(8,128)S(1)}, f32[512,4,128]{2,0,1:T(8,128)}, u32[]{:S(2)}) copy-start(f32[512,4,128]{2,0,1:T(8,128)} %copy.98) | copy-start | bytes 3145732
  128.0 19.4 %collective-permute-start.7 = (bf16[3,4,128,128]{2,3,0,1:T(8,128)(2,1)}, bf16[3,4,128,128]{2,3,0,1:T(8,128)(2,1)S(1)}, u32[]{:S(2)}, u32[]{:S(2)}) collective-permute-start(bf16[3,4,128,128]{2,3,0,1:T(8,128)(2,1)} %pad_maximum_fusion.1), channel_id=1, source_target_pairs={{0,32},{32,0},{8,40},{40,8},{16,48},{48,16},{24,56},{56,24},{64,96... | collective-permute-start | bytes 1179656 | tf_op jit(solution)/shard_map/ppermute | solution.py:14
  131.9 36.5 %all-to-all-start.3 = ((bf16[8,64,512]{2,1,0:T(8,128)(2,1)}), bf16[8,64,512]{2,1,0:T(8,128)(2,1)}, u32[]{:S(2)}, u32[]{:S(2)}) async-start(bf16[8,64,512]{2,1,0:T(8,128)(2,1)} %convert_element_type.688), calls=%async_computation.3 | async-start | bytes 1048576 | tf_op jit(solution)/shard_map/all_to_all | solution.py:169
  147.3 5.4 %copy-start = (bf16[4,512,512]{2,1,0:T(8,128)(2,1)S(1)}, bf16[4,512,512]{2,1,0:T(8,128)(2,1)}, u32[]{:S(2)}) copy-start(bf16[4,512,512]{2,1,0:T(8,128)(2,1)} %multiply_convert_fusion.1) | copy-start | bytes 6291460
  149.6 15.6 %collective-permute-start.8 = (bf16[2,4,128,128]{2,3,0,1:T(8,128)(2,1)}, bf16[2,4,128,128]{2,3,0,1:T(8,128)(2,1)}, u32[]{:S(2)}, u32[]{:S(2)}) collective-permute-start(bf16[2,4,128,128]{2,3,0,1:T(8,128)(2,1)} %pad_maximum_fusion.2), channel_id=1, source_target_pairs={{0,64},{64,0},{8,72},{72,8},{16,80},{80,16},{24,88},{88,24},{32,96... | collective-permute-start | bytes 786440 | tf_op jit(solution)/shard_map/ppermute | solution.py:14
  167.1 10.7 %collective-permute-start.9 = (bf16[1,4,128,128]{2,3,0,1:T(8,128)(2,1)}, bf16[1,4,128,128]{2,3,0,1:T(8,128)(2,1)}, u32[]{:S(2)}, u32[]{:S(2)}) collective-permute-start(bf16[1,4,128,128]{2,3,0,1:T(8,128)(2,1)} %add_convert_fusion.1), channel_id=1, source_target_pairs={{0,128},{128,0},{8,136},{136,8},{16,144},{144,16},{24,152},{152,24... | collective-permute-start | bytes 393224 | tf_op jit(solution)/shard_map/ppermute | solution.py:14
  168.5 14.9 %all-to-all-start.5 = ((bf16[8,64,512]{2,1,0:T(8,128)(2,1)}), bf16[8,64,512]{2,1,0:T(8,128)(2,1)}, u32[]{:S(2)}, u32[]{:S(2)}) async-start(bf16[8,64,512]{2,1,0:T(8,128)(2,1)} %convert_element_type.691), calls=%async_computation.5 | async-start | bytes 1048576 | tf_op jit(solution)/shard_map/all_to_all | solution.py:170
  179.3 9.1 %copy-start.3 = (bf16[512,4,128]{2,1,0:T(4,128)(2,1)S(1)}, bf16[512,4,128]{2,1,0:T(4,128)(2,1)}, u32[]{:S(2)}) copy-start(bf16[512,4,128]{2,1,0:T(4,128)(2,1)} %copy-done.2) | copy-start | bytes 1572868
  183.3 14.5 %all-to-all-start.6 = ((bf16[8,64,512]{2,1,0:T(8,128)(2,1)}), bf16[8,64,512]{2,1,0:T(8,128)(2,1)}, u32[]{:S(2)}, u32[]{:S(2)}) async-start(bf16[8,64,512]{2,1,0:T(8,128)(2,1)} %all_to_all.118), calls=%async_computation.6 | async-start | bytes 1048576 | tf_op jit(solution)/shard_map/all_to_all | solution.py:171
  197.8 13.7 %all-to-all-start.7 = ((bf16[8,64,512]{2,1,0:T(8,128)(2,1)}), bf16[8,64,512]{2,1,0:T(8,128)(2,1)S(1)}, u32[]{:S(2)}, u32[]{:S(2)}) async-start(bf16[8,64,512]{2,1,0:T(8,128)(2,1)} %all_to_all.122), calls=%async_computation.7 | async-start | bytes 1048576 | tf_op jit(solution)/shard_map/all_to_all | solution.py:172
where the time goes:
time: 214 us; the launch traced here: 212 us
  waiting for transfers between devices  73.3 us (34%)
  starting transfers between devices  63.8 us (30%)
  local copies, waits for them, and re-layouts  32.1 us (15%)
  matrix products  29.9 us (14%)
  other arithmetic  12.1 us (6%)
    ppermute x10, waiting for transfers between devices, swapped(): return lax.ppermute(block, axis, route)  35.7 us
    ppermute x10, starting transfers between devices, swapped(): return lax.ppermute(block, axis, route)  19.5 us
    all_to_all x1, starting transfers between devices, on_device(): lax.all_to_all(attended, 'head', split_axis=0, concat_axis=1, tiled=True)  9.64 us
    all_to_all x1, waiting for transfers between devices, on_device(): lax.all_to_all(value_input, 'head', split_axis=1, concat_axis=0, tiled=True)  8.33 us
    dot_general x1, matrix products, row_step(): jnp.einsum('phe,she->hps', cot_heads, value_heads, preferred_element_type...  7.41 us
    all_to_all x1, waiting for transfers between devices, on_device(): lax.all_to_all(key_input, 'head', split_axis=1, concat_axis=0, tiled=True)  6.93 us
    all_to_all x1, starting transfers between devices, on_device(): lax.all_to_all(value_input, 'head', split_axis=1, concat_axis=0, tiled=True)  6.73 us
    all_to_all x1, waiting for transfers between devices, on_device(): lax.all_to_all(cotangent, 'head', split_axis=1, concat_axis=0, tiled=True)  6.63 us
  transfers between devices with their start and end apart: 18, of which 14 were waited for; matrix products, arithmetic and copies ran while one was open for 30% of the time, Pallas kernels for 0%

commit v1 on v0

--- a/solution.py
+++ b/solution.py
@@ -1,7 +1,19 @@
+import functools
 import jax
 import jax.numpy as jnp
 from jax import lax
 from jax.sharding import PartitionSpec as P
+
+
+def show_points(view, device_axis, pos_dim, at_axis):
+    base_arr = lax.all_to_all(
+        jnp.stack(jnp.split(view, lax.axis_size(device_axis), pos_dim), 0), device_axis, 0, 0
+    )
+    shaped = jnp.concatenate(base_arr, at_axis)
+    return shaped
+
+
+pipes_keep_up = functools.partial(show_points, device_axis="head", pos_dim=1, at_axis=0)
 
 
 def swapped(block, axis, stride):
@@ -33,7 +45,7 @@
         lax.all_to_all(query_input, "head", split_axis=1, concat_axis=0, tiled=True),
         lax.all_to_all(key_input, "head", split_axis=1, concat_axis=0, tiled=True),
         lax.all_to_all(value_input, "head", split_axis=1, concat_axis=0, tiled=True),
-        lax.all_to_all(cotangent, "head", split_axis=1, concat_axis=0, tiled=True),
+        pipes_keep_up(cotangent),
     )
     head_count = level_codes.shape[0]
     total_levels = level_codes.shape[1]

time: 214 us -> 213 us (level)
  waiting for transfers between devices: 73.3 us -> 66.8 us
  local copies, waits for them, and re-layouts: 32.1 us -> 37.3 us
    all_to_all x1, waiting for transfers between devices: 8.33 us -> 3.74 us  [on_device(): lax.all_to_all(value_input, 'head', split_axis=1, concat_axis=0, tiled=True)]
    unnamed x66 -> x75, local copies, waits for them, and re-layouts: 1.66 us -> 6.08 us
  transfers between devices with their start and end apart: 18 -> 18, of which waited for: 14 -> 14; matrix products, arithmetic and copies ran while one was open for 30% -> 33% of each run, Pallas kernels for 0% -> 0%
where the time goes in v1:
time: 213 us; the launch traced here: 211 us
  waiting for transfers between devices  66.8 us (31%)
  starting transfers between devices  63.6 us (30%)
  local copies, waits for them, and re-layouts  37.3 us (18%)
  matrix products  29 us (14%)
  other arithmetic  13.4 us (6%)
    ppermute x10, waiting for transfers between devices, swapped(): return lax.ppermute(block, axis, route)  35.7 us
    ppermute x10, starting transfers between devices, swapped(): return lax.ppermute(block, axis, route)  19.5 us
    all_to_all x1, starting transfers between devices, on_device(): lax.all_to_all(attended, 'head', split_axis=0, concat_axis=1, tiled=True)  9.62 us
    dot_general x1, matrix products, row_step(): jnp.einsum('phd,shd->hps', query_heads, key_heads, preferred_element_type...  6.81 us
    all_to_all x1, waiting for transfers between devices, on_device(): lax.all_to_all(key_input, 'head', split_axis=1, concat_axis=0, tiled=True)  6.62 us
    all_to_all x1, starting transfers between devices, on_device(): lax.all_to_all(value_input, 'head', split_axis=1, concat_axis=0, tiled=True)  6.6 us
    dot_general x1, matrix products, row_step(): jnp.einsum('phe,she->hps', cot_heads, value_heads, preferred_element_type...  6.55 us
    all_to_all x1, waiting for transfers between devices, on_device(): lax.all_to_all(grad_key, 'head', split_axis=0, concat_axis=1, tiled=True)  6.28 us
  transfers between devices with their start and end apart: 18, of which 14 were waited for; matrix products, arithmetic and copies ran while one was open for 33% of the time, Pallas kernels for 0%

profile of v1, /device:TPU:1, one launch (start us, length us, event | category | flops | bytes accessed | tf_op | source)
XLA Modules:
  0.0 211.3 jit_solution(2539490356993156743)
XLA Ops:
  0.7 2.0 copy.176
  2.6 6.6 %all-to-all-start.2 = ((bf16[64,8,512]{2,0,1:T(8,128)(2,1)}), bf16[64,8,512]{2,0,1:T(8,128)(2,1)S(1)}, u32[]{:S(2)}, u32[]{:S(2)}) async-start(bf16[64,8,512]{2,0,1:T(8,128)(2,1)} %bitcast.147), calls=%async_computation.2 | async-start | bytes 1048576 | tf_op jit(solution)/shard_map/all_to_all | solution.py:47
  9.2 0.8 iota_compare_fusion.1
  12.8 0.8 copy.177
  14.9 3.7 %all-to-all-done.2 = bf16[64,8,512]{2,0,1:T(8,128)(2,1)S(1)} async-done(((bf16[64,8,512]{2,0,1:T(8,128)(2,1)}), bf16[64,8,512]{2,0,1:T(8,128)(2,1)S(1)}, u32[]{:S(2)}, u32[]{:S(2)}) %all-to-all-start.2) | async-done | bytes 524320 | tf_op jit(solution)/shard_map/all_to_all | solution.py:47
  18.6 4.4 %all-to-all-start.1 = ((bf16[64,8,512]{2,0,1:T(8,128)(2,1)}), bf16[64,8,512]{2,0,1:T(8,128)(2,1)S(1)}, u32[]{:S(2)}, u32[]{:S(2)}) async-start(bf16[64,8,512]{2,0,1:T(8,128)(2,1)} %bitcast.148), calls=%async_computation.1 | async-start | bytes 1048576 | tf_op jit(solution)/shard_map/all_to_all | solution.py:46
  23.6 0.8 copy.178
  25.7 6.6 %all-to-all-done.1 = bf16[64,8,512]{2,0,1:T(8,128)(2,1)S(1)} async-done(((bf16[64,8,512]{2,0,1:T(8,128)(2,1)}), bf16[64,8,512]{2,0,1:T(8,128)(2,1)S(1)}, u32[]{:S(2)}, u32[]{:S(2)}) %all-to-all-start.1) | async-done | bytes 524320 | tf_op jit(solution)/shard_map/all_to_all | solution.py:46
  32.4 4.4 %all-to-all-start.4 = ((bf16[8,64,512]{2,1,0:T(8,128)(2,1)}), bf16[8,64,512]{2,1,0:T(8,128)(2,1)S(1)}, u32[]{:S(2)}, u32[]{:S(2)}) async-start(bf16[8,64,512]{2,1,0:T(8,128)(2,1)} %bitcast_dynamic-update-slice_fusion), calls=%async_computation.4 | async-start | bytes 1048576 | tf_op jit(solution)/shard_map/all_to_all | solution.py:9
  36.7 3.9 %broadcast_compare_fusion.9 = (pred[512,512]{1,0:T(8,128)(4,1)}, pred[512,512]{1,0:T(8,128)(4,1)}, pred[512,512]{1,0:T(8,128)(4,1)}, pred[512,512]{1,0:T(8,128)(...) fusion(s32[512]{0:T(512)S(1)} %get-tuple-element.70, ...), kind=kLoop, calls=%fused_computation.44 | loop fusion | flops 9437184 | bytes 2637824 | tf_op jit(solution)/shard_map/while/body/eval_jaxpr/eq | solution.py:116
  40.6 5.5 %all-to-all-done.4 = bf16[8,64,512]{2,1,0:T(8,128)(2,1)S(1)} async-done(((bf16[8,64,512]{2,1,0:T(8,128)(2,1)}), bf16[8,64,512]{2,1,0:T(8,128)(2,1)S(1)}, u32[]{:S(2)}, u32[]{:S(2)}) %all-to-all-start.4) | async-done | bytes 524320 | tf_op jit(solution)/shard_map/all_to_all | solution.py:9
  46.1 4.4 %all-to-all-start = ((bf16[64,8,512]{2,0,1:T(8,128)(2,1)}), bf16[64,8,512]{2,0,1:T(8,128)(2,1)S(1)}, u32[]{:S(2)}, u32[]{:S(2)}) async-start(bf16[64,8,512]{2,0,1:T(8,128)(2,1)} %bitcast.149), calls=%async_computation | async-start | bytes 1048576 | tf_op jit(solution)/shard_map/all_to_all | solution.py:45
  51.2 1.1 copy.112
  52.4 1.3 copy.105
  54.0 1.0 fusion.87
  55.4 4.4 %all-to-all-done = bf16[64,8,512]{2,0,1:T(8,128)(2,1)S(1)} async-done(((bf16[64,8,512]{2,0,1:T(8,128)(2,1)}), bf16[64,8,512]{2,0,1:T(8,128)(2,1)S(1)}, u32[]{:S(2)}, u32[]{:S(2)}) %all-to-all-start) | async-done | bytes 524320 | tf_op jit(solution)/shard_map/all_to_all | solution.py:45
  59.8 0.9 reshape.3021
  60.9 6.8 %multiply_convert_fusion.2 = bf16[4,512,512]{2,1,0:T(8,128)(2,1)S(1)} fusion(f32[4,512]{1,0:T(4,128)S(1)} %get-tuple-element.47, f32[4,512]{1,0:T(4,128)} %get-tuple-element.48, f32[4,512]{1,0:T(4,128)} %get-tuple-element.49, f32[4,512]{1,0:T(4,128)} %get-tuple-element.50, f32[4,512]{1,0:T(4,128)} %get-tuple-element.51, f32[4,512]{1,0:T(4,128)} %get-tuple-element.52, ...), kind=kOutput, calls=%fused_computation.6 | convolution fusion | flops 283115520 | bytes 6111232 | tf_op jit(solution)/shard_map/while/body/eval_jaxpr/phd,shd->hps/dot_general | solution.py:121
  68.0 6.6 %multiply_convert_fusion.1 = bf16[4,512,512]{2,1,0:T(8,128)(2,1)} fusion(bf16[512,4,128]{0,2,1:T(8,128)(2,1)S(1)} %copy-done.5, f32[4,512]{1,0:T(4,128)S(1)} %get-tuple-element.47, f32[4,512]{1,0:T(4,128)S(1)} %copy-done.26, f32[4,512]{1,0:T(4,128)S(1)} %copy-done.27, f32[4,512]{1,0:T(4,128)S(1)} %copy-done.28, f32[4,512]{1,0:T(4,128)S(1)} %copy-done.29, ...), kind=kOutput, calls=%fused_computation.5 | convolution fusion | flops 283115520 | bytes 6111232 | tf_op jit(solution)/shard_map/while/body/eval_jaxpr/phe,she->hps/dot_general | solution.py:128
  74.5 0.9 fusion.88
  76.0 2.7 %collective-permute-start.1 = (bf16[4,128,128]{2,1,0:T(8,128)(2,1)S(1)}, bf16[4,128,128]{2,1,0:T(8,128)(2,1)S(1)}, u32[]{:S(2)}, u32[]{:S(2)}) collective-permute-start(bf16[4,128,128]{2,1,0:T(8,128)(2,1)S(1)} %fusion.38), channel_id=1, source_target_pairs={{0,16},{16,0},{8,24},{24,8},{32,48},{48,32},{40,56},{56,40},{64,80... | collective-permute-start | bytes 393224 | tf_op jit(solution)/shard_map/ppermute | solution.py:26
  78.7 16.2 %collective-permute-done.1 = bf16[4,128,128]{2,1,0:T(8,128)(2,1)S(1)} collective-permute-done((bf16[4,128,128]{2,1,0:T(8,128)(2,1)S(1)}, bf16[4,128,128]{2,1,0:T(8,128)(2,1)S(1)}, u32[]{:S(2)}, u32[]{:S(2)}) %collective-permute-start.1) | collective-permute-done | bytes 131104 | tf_op jit(solution)/shard_map/ppermute | solution.py:26
  95.0 1.7 collective-permute-start.2
  96.8 2.3 %collective-permute-done.2 = bf16[4,128,128]{2,1,0:T(8,128)(2,1)S(1)} collective-permute-done((bf16[4,128,128]{2,1,0:T(8,128)(2,1)S(1)}, bf16[4,128,128]{2,1,0:T(8,128)(2,1)S(1)}, u32[]{:S(2)}, u32[]{:S(2)}) %collective-permute-start.2) | collective-permute-done | bytes 131104 | tf_op jit(solution)/shard_map/ppermute | solution.py:26
  99.2 3.1 %collective-permute-start.3 = (bf16[4,128,128]{2,1,0:T(8,128)(2,1)S(1)}, bf16[4,128,128]{2,1,0:T(8,128)(2,1)S(1)}, u32[]{:S(2)}, u32[]{:S(2)}) collective-permute-start(bf16[4,128,128]{2,1,0:T(8,128)(2,1)S(1)} %fusion.39), channel_id=1, source_target_pairs={{0,64},{64,0},{8,72},{72,8},{16,80},{80,16},{24,88},{88,24},{32,96... | collective-permute-start | bytes 393224 | tf_op jit(solution)/shard_map/ppermute | solution.py:26
  102.3 3.7 %collective-permute-done.3 = bf16[4,128,128]{2,1,0:T(8,128)(2,1)S(1)} collective-permute-done((bf16[4,128,128]{2,1,0:T(8,128)(2,1)S(1)}, bf16[4,128,128]{2,1,0:T(8,128)(2,1)S(1)}, u32[]{:S(2)}, u32[]{:S(2)}) %collective-permute-start.3) | collective-permute-done | bytes 131104 | tf_op jit(solution)/shard_map/ppermute | solution.py:26
  106.1 6.2 %collective-permute-start.4 = (bf16[4,128,128]{2,1,0:T(8,128)(2,1)S(1)}, bf16[4,128,128]{2,1,0:T(8,128)(2,1)S(1)}, u32[]{:S(2)}, u32[]{:S(2)}) collective-permute-start(bf16[4,128,128]{2,1,0:T(8,128)(2,1)S(1)} %fusion.34), channel_id=1, source_target_pairs={{0,128},{128,0},{8,136},{136,8},{16,144},{144,16},{24,152},{152,24... | collective-permute-start | bytes 393224 | tf_op jit(solution)/shard_map/ppermute | solution.py:26
  113.2 0.9 pad_maximum_fusion
  114.8 0.8 copy-done.25
  115.7 1.9 fusion.1
  117.6 2.5 %copy.92 = f32[512,4,128]{2,0,1:T(8,128)} copy(f32[512,4,128]{0,2,1:T(8,128)} %fusion.1) | data formatting | bytes 2097152 | tf_op jit(solution)/shard_map/reduce_sum | solution.py:149
  120.1 4.5 %collective-permute-done.6 = bf16[4,4,128,128]{2,3,0,1:T(8,128)(2,1)} collective-permute-done((bf16[4,4,128,128]{2,3,0,1:T(8,128)(2,1)}, bf16[4,4,128,128]{2,3,0,1:T(8,128)(2,1)}, u32[]{:S(2)}, u32[]{:S(2)}) %collective-permute-start.6) | collective-permute-done | bytes 524320 | tf_op jit(solution)/shard_map/ppermute | solution.py:26
  124.6 1.5 add_convert_fusion.3
  126.1 0.8 pad_maximum_fusion.1
  127.6 1.2 copy.93
  128.8 2.0 convert_element_type.691
  130.9 9.6 %all-to-all-start.3 = ((bf16[8,64,512]{2,1,0:T(8,128)(2,1)}), bf16[8,64,512]{2,1,0:T(8,128)(2,1)}, u32[]{:S(2)}, u32[]{:S(2)}) async-start(bf16[8,64,512]{2,1,0:T(8,128)(2,1)} %convert_element_type.691), calls=%async_computation.3 | async-start | bytes 1048576 | tf_op jit(solution)/shard_map/all_to_all | solution.py:181
  140.5 3.2 %fusion = f32[512,4,128]{0,2,1:T(8,128)} fusion(f32[5,512,4]{1,0,2:T(8,128)} %copy.87, bf16[5,4,128,128]{3,2,1,0:T(8,128)(2,1)} %copy-done.25, bf16[512,4,128,1]{2,1,0,3:T(4,128)(2,1)} %bitcast.150), kind=kOutput, calls=%fused_computation.1 | convolution fusion | flops 337903616 | bytes 2269184 | tf_op jit(solution)/shard_map/phe,bhde->bphd/dot_general | solution.py:156
  143.7 2.5 %copy.100 = f32[512,4,128]{2,0,1:T(8,128)} copy(f32[512,4,128]{0,2,1:T(8,128)} %fusion) | data formatting | bytes 2097152 | tf_op jit(solution)/shard_map/reduce_sum | solution.py:154
  146.2 1.6 add_convert_fusion.2
  148.5 3.1 %collective-permute-start.8 = (bf16[2,4,128,128]{2,3,0,1:T(8,128)(2,1)}, bf16[2,4,128,128]{2,3,0,1:T(8,128)(2,1)}, u32[]{:S(2)}, u32[]{:S(2)}) collective-permute-start(bf16[2,4,128,128]{2,3,0,1:T(8,128)(2,1)} %pad_maximum_fusion.2), channel_id=1, source_target_pairs={{0,64},{64,0},{8,72},{72,8},{16,80},{80,16},{24,88},{88,24},{32,96... | collective-permute-start | bytes 786440 | tf_op jit(solution)/shard_map/ppermute | solution.py:26
  151.6 2.0 fusion.9
  153.6 1.2 copy.101
  154.8 2.0 convert_element_type.694
  156.8 7.3 %collective-permute-done.8 = bf16[2,4,128,128]{2,3,0,1:T(8,128)(2,1)} collective-permute-done((bf16[2,4,128,128]{2,3,0,1:T(8,128)(2,1)}, bf16[2,4,128,128]{2,3,0,1:T(8,128)(2,1)}, u32[]{:S(2)}, u32[]{:S(2)}) %collective-permute-start.8) | collective-permute-done | bytes 262176 | tf_op jit(solution)/shard_map/ppermute | solution.py:26
  164.1 1.9 add_convert_fusion.1
  166.0 1.4 collective-permute-start.9
  167.4 5.4 %all-to-all-start.5 = ((bf16[8,64,512]{2,1,0:T(8,128)(2,1)}), bf16[8,64,512]{2,1,0:T(8,128)(2,1)}, u32[]{:S(2)}, u32[]{:S(2)}) async-start(bf16[8,64,512]{2,1,0:T(8,128)(2,1)} %convert_element_type.694), calls=%async_computation.5 | async-start | bytes 1048576 | tf_op jit(solution)/shard_map/all_to_all | solution.py:182
  172.8 2.6 %convolution_bitcast_fusion = f32[512,4,128]{2,0,1:T(8,128)S(1)} fusion(bf16[4,512,512]{2,1,0:T(8,128)(2,1)} %multiply_convert_fusion.1, bf16[512,4,128]{2,1,0:T(4,128)(2,1)} %reshape.3021), kind=kOutput, calls=%fused_computation.12 | convolution fusion | flops 268435456 | bytes 3670016 | tf_op jit(solution)/shard_map/while/body/eval_jaxpr/hps,phd->shd/dot_general | solution.py:135
  175.3 1.4 collective-permute-done.9
  176.7 1.5 fusion.12
  178.2 1.2 copy.110
  179.4 2.0 all_to_all.107
  181.4 0.8 all-to-all-done.5
  182.2 5.0 %all-to-all-start.6 = ((bf16[8,64,512]{2,1,0:T(8,128)(2,1)}), bf16[8,64,512]{2,1,0:T(8,128)(2,1)}, u32[]{:S(2)}, u32[]{:S(2)}) async-start(bf16[8,64,512]{2,1,0:T(8,128)(2,1)} %all_to_all.107), calls=%async_computation.6 | async-start | bytes 1048576 | tf_op jit(solution)/shard_map/all_to_all | solution.py:183
  187.7 1.4 fusion.13
  189.4 1.0 all_to_all.111
  190.4 6.3 %all-to-all-done.6 = bf16[8,64,512]{2,1,0:T(8,128)(2,1)} async-done(((bf16[8,64,512]{2,1,0:T(8,128)(2,1)}), bf16[8,64,512]{2,1,0:T(8,128)(2,1)}, u32[]{:S(2)}, u32[]{:S(2)}) %all-to-all-start.6) | async-done | bytes 524320 | tf_op jit(solution)/shard_map/all_to_all | solution.py:183
  196.7 4.4 %all-to-all-start.7 = ((bf16[8,64,512]{2,1,0:T(8,128)(2,1)}), bf16[8,64,512]{2,1,0:T(8,128)(2,1)S(1)}, u32[]{:S(2)}, u32[]{:S(2)}) async-start(bf16[8,64,512]{2,1,0:T(8,128)(2,1)} %all_to_all.111), calls=%async_computation.7 | async-start | bytes 1048576 | tf_op jit(solution)/shard_map/all_to_all | solution.py:184
  201.1 1.9 copy.133
  203.0 1.9 copy.134
  204.8 1.9 copy.135
  206.7 3.7 %all-to-all-done.7 = bf16[8,64,512]{2,1,0:T(8,128)(2,1)S(1)} async-done(((bf16[8,64,512]{2,1,0:T(8,128)(2,1)}), bf16[8,64,512]{2,1,0:T(8,128)(2,1)S(1)}, u32[]{:S(2)}, u32[]{:S(2)}) %all-to-all-start.7) | async-done | bytes 524320 | tf_op jit(solution)/shard_map/all_to_all | solution.py:184
  210.5 0.8 copy.136
  (113 shorter events, 12.2 us)
Async XLA Ops:
  0.6 9.4 %copy-start.23 = (s32[4,15,512]{2,0,1:T(4,128)S(1)}, s32[4,15,512]{2,0,1:T(4,128)}, u32[]{:S(2)}) copy-start(s32[4,15,512]{2,0,1:T(4,128)} %param.9) | copy-start | bytes 368644
  0.6 9.5 %copy-start.9 = (bf16[64,4096]{1,0:T(8,128)(2,1)S(1)}, bf16[64,4096]{1,0:T(8,128)(2,1)}, u32[]{:S(2)}) copy-start(bf16[64,4096]{1,0:T(8,128)(2,1)} %param.8) | copy-start | bytes 1572868
  0.7 12.1 %copy-start.10 = (bf16[64,4096]{1,0:T(8,128)(2,1)S(1)}, bf16[64,4096]{1,0:T(8,128)(2,1)}, u32[]{:S(2)}) copy-start(bf16[64,4096]{1,0:T(8,128)(2,1)} %param.6) | copy-start | bytes 1572868
  2.6 16.0 %all-to-all-start.2 = ((bf16[64,8,512]{2,0,1:T(8,128)(2,1)}), bf16[64,8,512]{2,0,1:T(8,128)(2,1)S(1)}, u32[]{:S(2)}, u32[]{:S(2)}) async-start(bf16[64,8,512]{2,0,1:T(8,128)(2,1)} %bitcast.147), calls=%async_computation.2 | async-start | bytes 1048576 | tf_op jit(solution)/shard_map/all_to_all | solution.py:47
  9.2 14.4 %copy-start.11 = (bf16[64,4096]{1,0:T(8,128)(2,1)S(1)}, bf16[64,4096]{1,0:T(8,128)(2,1)}, u32[]{:S(2)}) copy-start(bf16[64,4096]{1,0:T(8,128)(2,1)} %param.5) | copy-start | bytes 1572868
  18.6 13.7 %all-to-all-start.1 = ((bf16[64,8,512]{2,0,1:T(8,128)(2,1)}), bf16[64,8,512]{2,0,1:T(8,128)(2,1)S(1)}, u32[]{:S(2)}, u32[]{:S(2)}) async-start(bf16[64,8,512]{2,0,1:T(8,128)(2,1)} %bitcast.148), calls=%async_computation.1 | async-start | bytes 1048576 | tf_op jit(solution)/shard_map/all_to_all | solution.py:46
  32.4 13.7 %all-to-all-start.4 = ((bf16[8,64,512]{2,1,0:T(8,128)(2,1)}), bf16[8,64,512]{2,1,0:T(8,128)(2,1)S(1)}, u32[]{:S(2)}, u32[]{:S(2)}) async-start(bf16[8,64,512]{2,1,0:T(8,128)(2,1)} %bitcast_dynamic-update-slice_fusion), calls=%async_computation.4 | async-start | bytes 1048576 | tf_op jit(solution)/shard_map/all_to_all | solution.py:9
  46.1 13.7 %all-to-all-start = ((bf16[64,8,512]{2,0,1:T(8,128)(2,1)}), bf16[64,8,512]{2,0,1:T(8,128)(2,1)S(1)}, u32[]{:S(2)}, u32[]{:S(2)}) async-start(bf16[64,8,512]{2,0,1:T(8,128)(2,1)} %bitcast.149), calls=%async_computation | async-start | bytes 1048576 | tf_op jit(solution)/shard_map/all_to_all | solution.py:45
  51.2 2.6 %copy-start.2 = (bf16[512,4,128]{2,1,0:T(4,128)(2,1)}, bf16[512,4,128]{2,1,0:T(4,128)(2,1)S(1)}, u32[]{:S(2)}) copy-start(bf16[512,4,128]{2,1,0:T(4,128)(2,1)S(1)} %reshape_reshape.3) | copy-start | bytes 1572868
  55.0 21.0 %collective-permute-start = (bf16[4,128,128]{2,1,0:T(8,128)(2,1)}, bf16[4,128,128]{2,1,0:T(8,128)(2,1)S(1)}, u32[]{:S(2)}, u32[]{:S(2)}) collective-permute-start(bf16[4,128,128]{2,1,0:T(8,128)(2,1)} %get-tuple-element.66), channel_id=1, source_target_pairs={{0,8},{8,0},{16,24},{24,16},{32,40},{40,32},{48,56},{56,48},{64,72... | collective-permute-start | bytes 393224 | tf_op jit(solution)/shard_map/ppermute | solution.py:26
  60.8 7.0 %copy-start.5 = (bf16[512,4,128]{0,2,1:T(8,128)(2,1)S(1)}, bf16[512,4,128]{0,2,1:T(8,128)(2,1)}, u32[]{:S(2)}) copy-start(bf16[512,4,128]{0,2,1:T(8,128)(2,1)} %copy.112) | copy-start | bytes 1572868
  60.8 7.0 %copy-start.12 = (pred[512,512]{1,0:T(8,128)(4,1)S(1)}, pred[512,512]{1,0:T(8,128)(4,1)}, u32[]{:S(2)}) copy-start(pred[512,512]{1,0:T(8,128)(4,1)} %iota_compare_fusion.1) | copy-start | bytes 786436
  60.8 7.0 %copy-start.13 = (pred[512,512]{1,0:T(8,128)(4,1)S(1)}, pred[512,512]{1,0:T(8,128)(4,1)}, u32[]{:S(2)}) copy-start(pred[512,512]{1,0:T(8,128)(4,1)} %get-tuple-element.56) | copy-start | bytes 786436
  60.8 7.0 %copy-start.14 = (pred[512,512]{1,0:T(8,128)(4,1)S(1)}, pred[512,512]{1,0:T(8,128)(4,1)}, u32[]{:S(2)}) copy-start(pred[512,512]{1,0:T(8,128)(4,1)} %get-tuple-element.57) | copy-start | bytes 786436
  60.8 7.0 %copy-start.15 = (pred[512,512]{1,0:T(8,128)(4,1)S(1)}, pred[512,512]{1,0:T(8,128)(4,1)}, u32[]{:S(2)}) copy-start(pred[512,512]{1,0:T(8,128)(4,1)} %get-tuple-element.58) | copy-start | bytes 786436
  60.8 7.0 %copy-start.16 = (pred[512,512]{1,0:T(8,128)(4,1)S(1)}, pred[512,512]{1,0:T(8,128)(4,1)}, u32[]{:S(2)}) copy-start(pred[512,512]{1,0:T(8,128)(4,1)} %get-tuple-element.59) | copy-start | bytes 786436
  60.8 7.0 %copy-start.17 = (pred[512,512]{1,0:T(8,128)(4,1)S(1)}, pred[512,512]{1,0:T(8,128)(4,1)}, u32[]{:S(2)}) copy-start(pred[512,512]{1,0:T(8,128)(4,1)} %get-tuple-element.60) | copy-start | bytes 786436
  60.8 7.0 %copy-start.18 = (pred[512,512]{1,0:T(8,128)(4,1)S(1)}, pred[512,512]{1,0:T(8,128)(4,1)}, u32[]{:S(2)}) copy-start(pred[512,512]{1,0:T(8,128)(4,1)} %get-tuple-element.61) | copy-start | bytes 786436
  60.8 7.0 %copy-start.19 = (pred[512,512]{1,0:T(8,128)(4,1)S(1)}, pred[512,512]{1,0:T(8,128)(4,1)}, u32[]{:S(2)}) copy-start(pred[512,512]{1,0:T(8,128)(4,1)} %get-tuple-element.62) | copy-start | bytes 786436
  60.8 7.0 %copy-start.20 = (pred[512,512]{1,0:T(8,128)(4,1)S(1)}, pred[512,512]{1,0:T(8,128)(4,1)}, u32[]{:S(2)}) copy-start(pred[512,512]{1,0:T(8,128)(4,1)} %get-tuple-element.63) | copy-start | bytes 786436
  60.8 7.0 %copy-start.21 = (pred[512,512]{1,0:T(8,128)(4,1)S(1)}, pred[512,512]{1,0:T(8,128)(4,1)}, u32[]{:S(2)}) copy-start(pred[512,512]{1,0:T(8,128)(4,1)} %get-tuple-element.64) | copy-start | bytes 786436
  60.8 7.0 %copy-start.22 = (pred[512,512]{1,0:T(8,128)(4,1)S(1)}, pred[512,512]{1,0:T(8,128)(4,1)}, u32[]{:S(2)}) copy-start(pred[512,512]{1,0:T(8,128)(4,1)} %get-tuple-element.65) | copy-start | bytes 786436
  60.9 7.0 %copy-start.26 = (f32[4,512]{1,0:T(4,128)S(1)}, f32[4,512]{1,0:T(4,128)}, u32[]{:S(2)}) copy-start(f32[4,512]{1,0:T(4,128)} %get-tuple-element.48) | copy-start | bytes 24580
  60.9 7.0 %copy-start.27 = (f32[4,512]{1,0:T(4,128)S(1)}, f32[4,512]{1,0:T(4,128)}, u32[]{:S(2)}) copy-start(f32[4,512]{1,0:T(4,128)} %get-tuple-element.49) | copy-start | bytes 24580
  60.9 7.0 %copy-start.28 = (f32[4,512]{1,0:T(4,128)S(1)}, f32[4,512]{1,0:T(4,128)}, u32[]{:S(2)}) copy-start(f32[4,512]{1,0:T(4,128)} %get-tuple-element.50) | copy-start | bytes 24580
  60.9 7.0 %copy-start.29 = (f32[4,512]{1,0:T(4,128)S(1)}, f32[4,512]{1,0:T(4,128)}, u32[]{:S(2)}) copy-start(f32[4,512]{1,0:T(4,128)} %get-tuple-element.51) | copy-start | bytes 24580
  60.9 7.0 %copy-start.30 = (f32[4,512]{1,0:T(4,128)S(1)}, f32[4,512]{1,0:T(4,128)}, u32[]{:S(2)}) copy-start(f32[4,512]{1,0:T(4,128)} %get-tuple-element.52) | copy-start | bytes 24580
  60.9 7.0 %copy-start.31 = (f32[4,512]{1,0:T(4,128)S(1)}, f32[4,512]{1,0:T(4,128)}, u32[]{:S(2)}) copy-start(f32[4,512]{1,0:T(4,128)} %get-tuple-element.53) | copy-start | bytes 24580
  60.9 7.0 %copy-start.32 = (f32[4,512]{1,0:T(4,128)S(1)}, f32[4,512]{1,0:T(4,128)}, u32[]{:S(2)}) copy-start(f32[4,512]{1,0:T(4,128)} %get-tuple-element.54) | copy-start | bytes 24580
  60.9 7.0 %copy-start.33 = (f32[4,512]{1,0:T(4,128)S(1)}, f32[4,512]{1,0:T(4,128)}, u32[]{:S(2)}) copy-start(f32[4,512]{1,0:T(4,128)} %get-tuple-element.55) | copy-start | bytes 24580
  68.0 6.6 %copy-start.7 = (bf16[512,4,128]{2,1,0:T(4,128)(2,1)S(1)}, bf16[512,4,128]{2,1,0:T(4,128)(2,1)}, u32[]{:S(2)}) copy-start(bf16[512,4,128]{2,1,0:T(4,128)(2,1)} %reshape.3021) | copy-start | bytes 1572868
  68.0 6.6 %copy-start.8 = (f32[512,4,128]{0,2,1:T(8,128)S(1)}, f32[512,4,128]{0,2,1:T(8,128)}, u32[]{:S(2)}) copy-start(f32[512,4,128]{0,2,1:T(8,128)} %copy.105) | copy-start | bytes 3145732
  68.0 6.6 %copy-start.24 = (f32[5,512,4]{1,0,2:T(8,128)S(1)}, f32[5,512,4]{1,0,2:T(8,128)}, u32[]{:S(2)}) copy-start(f32[5,512,4]{1,0,2:T(8,128)} %copy.87) | copy-start | bytes 122884
  75.4 37.1 %copy-start.1 = (f32[5,4,128,128]{2,3,0,1:T(8,128)}, f32[5,4,128,128]{2,3,0,1:T(8,128)S(1)}, u32[]{:S(2)}) copy-start(f32[5,4,128,128]{2,3,0,1:T(8,128)S(1)} %get-tuple-element.69) | copy-start | bytes 3932164
  75.4 36.9 %collective-permute-start.5 = (bf16[5,4,128,128]{2,3,0,1:T(8,128)(2,1)S(1)}, bf16[5,4,128,128]{2,3,0,1:T(8,128)(2,1)S(1)}, u32[]{:S(2)}, u32[]{:S(2)}) collective-permute-start(bf16[5,4,128,128]{2,3,0,1:T(8,128)(2,1)S(1)} %get-tuple-element.68), channel_id=1, source_target_pairs={{0,8},{8,0},{16,24},{24,16},{32,40},{40,32},{48,56},{56,48},{64,72... | collective-permute-start | bytes 1966088 | tf_op jit(solution)/shard_map/ppermute | solution.py:26
  76.0 18.9 %collective-permute-start.1 = (bf16[4,128,128]{2,1,0:T(8,128)(2,1)S(1)}, bf16[4,128,128]{2,1,0:T(8,128)(2,1)S(1)}, u32[]{:S(2)}, u32[]{:S(2)}) collective-permute-start(bf16[4,128,128]{2,1,0:T(8,128)(2,1)S(1)} %fusion.38), channel_id=1, source_target_pairs={{0,16},{16,0},{8,24},{24,8},{32,48},{48,32},{40,56},{56,40},{64,80... | collective-permute-start | bytes 393224 | tf_op jit(solution)/shard_map/ppermute | solution.py:26
  95.0 4.1 %collective-permute-start.2 = (bf16[4,128,128]{2,1,0:T(8,128)(2,1)S(1)}, bf16[4,128,128]{2,1,0:T(8,128)(2,1)S(1)}, u32[]{:S(2)}, u32[]{:S(2)}) collective-permute-start(bf16[4,128,128]{2,1,0:T(8,128)(2,1)S(1)} %fusion.85), channel_id=1, source_target_pairs={{0,32},{32,0},{8,40},{40,8},{16,48},{48,16},{24,56},{56,24},{64,96... | collective-permute-start | bytes 393224 | tf_op jit(solution)/shard_map/ppermute | solution.py:26
  99.2 6.8 %collective-permute-start.3 = (bf16[4,128,128]{2,1,0:T(8,128)(2,1)S(1)}, bf16[4,128,128]{2,1,0:T(8,128)(2,1)S(1)}, u32[]{:S(2)}, u32[]{:S(2)}) collective-permute-start(bf16[4,128,128]{2,1,0:T(8,128)(2,1)S(1)} %fusion.39), channel_id=1, source_target_pairs={{0,64},{64,0},{8,72},{72,8},{16,80},{80,16},{24,88},{88,24},{32,96... | collective-permute-start | bytes 393224 | tf_op jit(solution)/shard_map/ppermute | solution.py:26
  106.1 8.7 %collective-permute-start.4 = (bf16[4,128,128]{2,1,0:T(8,128)(2,1)S(1)}, bf16[4,128,128]{2,1,0:T(8,128)(2,1)S(1)}, u32[]{:S(2)}, u32[]{:S(2)}) collective-permute-start(bf16[4,128,128]{2,1,0:T(8,128)(2,1)S(1)} %fusion.34), channel_id=1, source_target_pairs={{0,128},{128,0},{8,136},{136,8},{16,144},{144,16},{24,152},{152,24... | collective-permute-start | bytes 393224 | tf_op jit(solution)/shard_map/ppermute | solution.py:26
  112.3 0.8 copy-start.4
  114.0 10.6 %collective-permute-start.6 = (bf16[4,4,128,128]{2,3,0,1:T(8,128)(2,1)}, bf16[4,4,128,128]{2,3,0,1:T(8,128)(2,1)}, u32[]{:S(2)}, u32[]{:S(2)}) collective-permute-start(bf16[4,4,128,128]{2,3,0,1:T(8,128)(2,1)} %pad_maximum_fusion), channel_id=1, source_target_pairs={{0,16},{16,0},{8,24},{24,8},{32,48},{48,32},{40,56},{56,40},{64,80... | collective-permute-start | bytes 1572872 | tf_op jit(solution)/shard_map/ppermute | solution.py:26
  114.8 0.8 copy-start.25
  120.1 6.8 %copy-start.3 = (f32[512,4,128]{2,0,1:T(8,128)S(1)}, f32[512,4,128]{2,0,1:T(8,128)}, u32[]{:S(2)}) copy-start(f32[512,4,128]{2,0,1:T(8,128)} %copy.92) | copy-start | bytes 3145732
  126.9 19.3 %collective-permute-start.7 = (bf16[3,4,128,128]{2,3,0,1:T(8,128)(2,1)}, bf16[3,4,128,128]{2,3,0,1:T(8,128)(2,1)S(1)}, u32[]{:S(2)}, u32[]{:S(2)}) collective-permute-start(bf16[3,4,128,128]{2,3,0,1:T(8,128)(2,1)} %pad_maximum_fusion.1), channel_id=1, source_target_pairs={{0,32},{32,0},{8,40},{40,8},{16,48},{48,16},{24,56},{56,24},{64,96... | collective-permute-start | bytes 1179656 | tf_op jit(solution)/shard_map/ppermute | solution.py:26
  130.9 36.5 %all-to-all-start.3 = ((bf16[8,64,512]{2,1,0:T(8,128)(2,1)}), bf16[8,64,512]{2,1,0:T(8,128)(2,1)}, u32[]{:S(2)}, u32[]{:S(2)}) async-start(bf16[8,64,512]{2,1,0:T(8,128)(2,1)} %convert_element_type.691), calls=%async_computation.3 | async-start | bytes 1048576 | tf_op jit(solution)/shard_map/all_to_all | solution.py:181
  146.2 5.4 %copy-start = (bf16[4,512,512]{2,1,0:T(8,128)(2,1)S(1)}, bf16[4,512,512]{2,1,0:T(8,128)(2,1)}, u32[]{:S(2)}) copy-start(bf16[4,512,512]{2,1,0:T(8,128)(2,1)} %multiply_convert_fusion.1) | copy-start | bytes 6291460
  148.5 15.6 %collective-permute-start.8 = (bf16[2,4,128,128]{2,3,0,1:T(8,128)(2,1)}, bf16[2,4,128,128]{2,3,0,1:T(8,128)(2,1)}, u32[]{:S(2)}, u32[]{:S(2)}) collective-permute-start(bf16[2,4,128,128]{2,3,0,1:T(8,128)(2,1)} %pad_maximum_fusion.2), channel_id=1, source_target_pairs={{0,64},{64,0},{8,72},{72,8},{16,80},{80,16},{24,88},{88,24},{32,96... | collective-permute-start | bytes 786440 | tf_op jit(solution)/shard_map/ppermute | solution.py:26
  166.0 10.7 %collective-permute-start.9 = (bf16[1,4,128,128]{2,3,0,1:T(8,128)(2,1)}, bf16[1,4,128,128]{2,3,0,1:T(8,128)(2,1)}, u32[]{:S(2)}, u32[]{:S(2)}) collective-permute-start(bf16[1,4,128,128]{2,3,0,1:T(8,128)(2,1)} %add_convert_fusion.1), channel_id=1, source_target_pairs={{0,128},{128,0},{8,136},{136,8},{16,144},{144,16},{24,152},{152,24... | collective-permute-start | bytes 393224 | tf_op jit(solution)/shard_map/ppermute | solution.py:26
  167.4 14.9 %all-to-all-start.5 = ((bf16[8,64,512]{2,1,0:T(8,128)(2,1)}), bf16[8,64,512]{2,1,0:T(8,128)(2,1)}, u32[]{:S(2)}, u32[]{:S(2)}) async-start(bf16[8,64,512]{2,1,0:T(8,128)(2,1)} %convert_element_type.694), calls=%async_computation.5 | async-start | bytes 1048576 | tf_op jit(solution)/shard_map/all_to_all | solution.py:182
  178.2 9.1 %copy-start.6 = (bf16[512,4,128]{0,2,1:T(8,128)(2,1)S(1)}, bf16[512,4,128]{0,2,1:T(8,128)(2,1)}, u32[]{:S(2)}) copy-start(bf16[512,4,128]{0,2,1:T(8,128)(2,1)} %copy.112) | copy-start | bytes 1572868
  182.2 14.5 %all-to-all-start.6 = ((bf16[8,64,512]{2,1,0:T(8,128)(2,1)}), bf16[8,64,512]{2,1,0:T(8,128)(2,1)}, u32[]{:S(2)}, u32[]{:S(2)}) async-start(bf16[8,64,512]{2,1,0:T(8,128)(2,1)} %all_to_all.107), calls=%async_computation.6 | async-start | bytes 1048576 | tf_op jit(solution)/shard_map/all_to_all | solution.py:183
  196.7 13.7 %all-to-all-start.7 = ((bf16[8,64,512]{2,1,0:T(8,128)(2,1)}), bf16[8,64,512]{2,1,0:T(8,128)(2,1)S(1)}, u32[]{:S(2)}, u32[]{:S(2)}) async-start(bf16[8,64,512]{2,1,0:T(8,128)(2,1)} %all_to_all.111), calls=%async_computation.7 | async-start | bytes 1048576 | tf_op jit(solution)/shard_map/all_to_all | solution.py:184
